TPU v7x, 32 devices: a whole 2x2x4 slice. The times are simulated.
32 devices in a mesh: tm: 4 (over y, x), space: 8 (over z, core).
Axes of the slice: x: 2, y: 2, z: 4, core: 2. Of those that a mesh axis runs over, the one named last changes fastest.
Arguments:
- residual_field: float32 [64, 128, 128, 128], P('tm', 'space'), may hold values from -6 to 6
- eigvec_x: float32 [128, 128], replicated, may hold values from -1 to 1, as said below
- eigvec_y: float32 [128, 128], replicated, may hold values from -1 to 1, as said below
- eigvec_z: float32 [128, 128], replicated, may hold values from -1 to 1, as said below
- eigval_x: float32 [128], replicated, may hold values from 0.0001 to 0.05
- eigval_y: float32 [128], replicated, may hold values from 0.0001 to 0.05
- eigval_z: float32 [128], replicated, may hold values from 0.0001 to 0.05
Outputs:
- update: float32 [64, 128, 128, 128], P('tm', 'space')
Inputs may be any that keep to these rules, and one draw needn't show every extreme that they name: `eigvec_x`: an orthogonal matrix. `eigvec_y`: an orthogonal matrix. `eigvec_z`: an orthogonal matrix.
All inputs are finite; a program needn't handle non-finite values.
Results may differ from a plain program's by a relative error of at most 0.00025.
Values sent between devices are 32-bit elements; how exact they have to be, the bound alone decides.
A program may use at most 256 MiB of HBM per device.

v0:
```python
import functools
import jax
import jax.numpy as jnp
from jax import lax
from jax.experimental import pallas as pl
from jax.experimental.pallas import tpu as pltpu
from jax.sharding import PartitionSpec as P

highest = lax.Precision.HIGHEST
circulant_alpha = 0.01
tile_rows = 8


def halves(a):
    high = a.astype(jnp.bfloat16)
    return high, (a - high.astype(jnp.float32)).astype(jnp.bfloat16)


def stacked(matrix):
    return jnp.concatenate(halves(matrix), axis=0)


def left_product(left, a):
    rows, columns = left.shape[0] // 2, a.shape[1]
    r = jnp.dot(left, jnp.concatenate(halves(a), axis=1), preferred_element_type=jnp.float32)
    return (r[:rows, :columns] + r[rows:, :columns]) + (r[:rows, columns:] + r[rows:, columns:])


def right_product(a, right):
    columns = right.shape[1] // 2
    r = jnp.dot(jnp.concatenate(halves(a), axis=1), right, preferred_element_type=jnp.float32)
    return r[:, :columns] + r[:, columns:]


def power(a, n):
    result = None
    while n:
        if n & 1:
            result = a if result is None else result * a
        a, n = a * a, n >> 1
    return result


def plane_kernel(a_ref, left_ref, right_ref, o_ref):
    left = stacked(left_ref[...])
    right = jnp.concatenate(halves(right_ref[...]), axis=1)
    right = jnp.concatenate([right, right], axis=0)

    def one(x, carry):
        o_ref[0, x] = left_product(left, right_product(a_ref[0, x], right))
        return carry

    lax.fori_loop(0, a_ref.shape[1], one, 0, unroll=4)


def plane_transform(a, left, right):
    steps, rows, size_y, size_z = a.shape
    block = pl.BlockSpec((1, rows, size_y, size_z), lambda t: (t, 0, 0, 0))
    whole = lambda m: pl.BlockSpec(m.shape, lambda t: (0, 0))
    return pl.pallas_call(
        plane_kernel,
        grid=(steps,),
        in_specs=[block, whole(left), whole(right)],
        out_specs=block,
        out_shape=jax.ShapeDtypeStruct(a.shape, jnp.float32),
        compiler_params=pltpu.CompilerParams(vmem_limit_bytes=60 * 2**20),
    )(a, left, right)


def exchange_kernel(
    space_count, time_count, chunks,
    in_ref, vt_ref, v_ref, ex_ref, shift_ref, out_ref,
    recv, fins, own_in, own_out, go_send, go_recv, back_send, back_recv, st_send, st_recv,
):
    steps, rows, band_rows = recv.shape[2], recv.shape[3], recv.shape[4]
    size_z = recv.shape[5]
    band = band_rows * chunks
    me = lax.axis_index("space")
    position = lax.axis_index("tm")

    def peer_of(k):
        return lax.rem(me + k, space_count)

    def timer_of(k):
        return lax.rem(position + k, time_count)

    def columns(owner, c):
        return pl.ds(pl.multiple_of(owner * band + c * band_rows, tile_rows), band_rows)

    def go(c, peer):
        return pltpu.make_async_remote_copy(
            src_ref=in_ref.at[:, :, columns(peer, c), :],
            dst_ref=recv.at[c, me],
            send_sem=go_send.at[c, peer],
            recv_sem=go_recv.at[c, me],
            device_id={"space": peer},
            device_id_type=pl.DeviceIdType.MESH,
        )

    def go_arrival(c, peer):
        return pltpu.make_async_remote_copy(
            src_ref=in_ref.at[:, :, columns(peer, c), :],
            dst_ref=recv.at[c, peer],
            send_sem=go_send.at[c, peer],
            recv_sem=go_recv.at[c, peer],
            device_id={"space": peer},
            device_id_type=pl.DeviceIdType.MESH,
        )

    def back(c, peer):
        return pltpu.make_async_remote_copy(
            src_ref=recv.at[c, peer],
            dst_ref=out_ref.at[:, :, columns(me, c), :],
            send_sem=back_send.at[c, peer],
            recv_sem=back_recv.at[c, me],
            device_id={"space": peer},
            device_id_type=pl.DeviceIdType.MESH,
        )

    def back_arrival(c, peer):
        return pltpu.make_async_remote_copy(
            src_ref=recv.at[c, peer],
            dst_ref=out_ref.at[:, :, columns(peer, c), :],
            send_sem=back_send.at[c, peer],
            recv_sem=back_recv.at[c, peer],
            device_id={"space": peer},
            device_id_type=pl.DeviceIdType.MESH,
        )

    def final(c, peer, owner):
        return pltpu.make_async_remote_copy(
            src_ref=fins.at[c, owner],
            dst_ref=fins.at[c, owner],
            send_sem=st_send.at[c, peer],
            recv_sem=st_recv.at[c, owner],
            device_id={"tm": peer},
            device_id_type=pl.DeviceIdType.MESH,
        )

    def take_own(c):
        return pltpu.make_async_copy(
            in_ref.at[:, :, columns(me, c), :], recv.at[c, me], own_in.at[c]
        )

    def give_own(c):
        return pltpu.make_async_copy(
            recv.at[c, me], out_ref.at[:, :, columns(me, c), :], own_out.at[c]
        )

    barrier = pltpu.get_barrier_semaphore()
    for k in range(1, space_count):
        pl.semaphore_signal(
            barrier, inc=1, device_id={"space": peer_of(k)}, device_id_type=pl.DeviceIdType.MESH
        )
    for k in range(1, time_count):
        pl.semaphore_signal(
            barrier, inc=1, device_id={"tm": timer_of(k)}, device_id_type=pl.DeviceIdType.MESH
        )
    pl.semaphore_wait(barrier, space_count + time_count - 2)

    middle = space_count // 2
    offsets = sorted(range(1, space_count), key=lambda k: abs(k - middle))
    for c in range(chunks):
        for k in offsets:
            go(c, peer_of(k)).start()
        take_own(c).start()

    left = stacked(vt_ref[...])
    left_back = stacked(v_ref[...])
    ex = ex_ref[...]

    def load(c, t, j):
        parts = [
            recv.at[c, s, t].reshape(rows * band_rows, size_z)[pl.ds(j, rows, stride=band_rows), :]
            for s in range(space_count)
        ]
        return jnp.concatenate(parts, axis=0)

    def store(c, t, j, value):
        for s in range(space_count):
            view = recv.at[c, s, t].reshape(rows * band_rows, size_z)
            view[pl.ds(j, rows, stride=band_rows), :] = value[s * rows : (s + 1) * rows]

    def chunk(c, carry):
        for k in offsets:
            go_arrival(c, peer_of(k)).wait_recv()
        take_own(c).wait()
        for j in range(band_rows):
            damping = 1.0 / (1.0 + (ex + shift_ref[c, j : j + 1, :]))

            def forward(t, state, j=j, damping=damping):
                state = damping * (state + left_product(left, load(c, t, j)))
                store(c, t, j, state)
                return state

            fins[c, position, j] = lax.fori_loop(
                0, steps, forward, jnp.zeros_like(damping), unroll=2
            )
        for k in range(1, time_count):
            final(c, timer_of(k), position).start()
        for k in range(1, time_count):
            final(c, timer_of(k), timer_of(k)).wait_recv()
        for j in range(band_rows):
            damping = 1.0 / (1.0 + (ex + shift_ref[c, j : j + 1, :]))
            block_decay = power(damping, steps)
            overall = fins[c, 0, j]
            for p in range(1, time_count):
                overall = block_decay * overall + fins[c, p, j]
            incoming = (circulant_alpha * overall) / (
                1.0 - circulant_alpha * power(block_decay, time_count)
            )
            for p in range(time_count - 1):
                incoming = jnp.where(
                    p < position, block_decay * incoming + fins[c, p, j], incoming
                )

            def inverse(t, incoming, j=j, damping=damping):
                incoming = damping * incoming
                store(c, t, j, left_product(left_back, load(c, t, j) + incoming))
                return incoming

            lax.fori_loop(0, steps, inverse, incoming, unroll=2)
        for k in offsets:
            go(c, peer_of(k)).wait_send()
            back(c, peer_of(k)).start()
        give_own(c).start()
        return carry

    lax.fori_loop(0, chunks, chunk, 0)

    for c in range(chunks):
        for k in range(1, time_count):
            final(c, timer_of(k), position).wait_send()
        for k in offsets:
            back(c, peer_of(k)).wait_send()
            back_arrival(c, peer_of(k)).wait_recv()
        give_own(c).wait()


def exchange_solve(planes, eigvec_x, eigval_x, shift_yz, space_count, time_count):
    steps, rows, size_y, size_z = planes.shape
    band = size_y // space_count
    chunks = 2 if band % (2 * tile_rows) == 0 else 1
    band_rows = band // chunks
    size_x = rows * space_count
    vmem = pl.BlockSpec(memory_space=pltpu.VMEM)
    dma = pltpu.SemaphoreType.DMA
    return pl.pallas_call(
        functools.partial(exchange_kernel, space_count, time_count, chunks),
        in_specs=[pl.BlockSpec(memory_space=pl.ANY)] + [vmem] * 4,
        out_specs=pl.BlockSpec(memory_space=pl.ANY),
        out_shape=jax.ShapeDtypeStruct(planes.shape, jnp.float32),
        scratch_shapes=[
            pltpu.VMEM((chunks, space_count, steps, rows, band_rows, size_z), jnp.float32),
            pltpu.VMEM((chunks, time_count, band_rows, size_x, size_z), jnp.float32),
            dma((chunks,)),
            dma((chunks,)),
            dma((chunks, space_count)),
            dma((chunks, space_count)),
            dma((chunks, space_count)),
            dma((chunks, space_count)),
            dma((chunks, time_count)),
            dma((chunks, time_count)),
        ],
        compiler_params=pltpu.CompilerParams(
            collective_id=0, has_side_effects=True, vmem_limit_bytes=60 * 2**20
        ),
    )(
        planes,
        eigvec_x.T,
        eigvec_x,
        jnp.broadcast_to(eigval_x[:, None], (size_x, size_z)),
        shift_yz.reshape(chunks, band_rows, size_z),
    )


def entering(part, axis, combine, identity):
    place = lax.axis_index(axis)
    gathered = jax.tree.map(lambda a: lax.all_gather(a, axis), part)
    state = jax.tree.map(lambda a, e: jnp.zeros_like(a) + jnp.asarray(e, a.dtype), part, identity)

    def one(step, state):
        return combine(
            state, jax.tree.map(lambda a: lax.dynamic_index_in_dim(a, step, 0, False), gathered)
        )

    return lax.fori_loop(0, place, one, state)


def recurrence_solve(values, shifts, time_count):
    steps_local = values.shape[0]
    damping = 1.0 / (1.0 + shifts)

    def advance(running, step_row):
        running = damping * (running + step_row)
        return (running, running)

    final_state, partial_value = lax.scan(advance, jnp.zeros_like(shifts), values)
    block_decay = damping**steps_local
    position = lax.axis_index("tm")

    def compose(early_map, late_map):
        return (early_map[0] * late_map[0], late_map[0] * early_map[1] + late_map[1])

    lead_power, offset = entering(
        (block_decay, final_state), "tm", compose, (jnp.ones_like(shifts), jnp.zeros_like(shifts))
    )
    tail_power = jnp.power(block_decay, (time_count - 1 - position).astype(jnp.float32))
    overall = lax.psum(tail_power * final_state, "tm")
    start_value = circulant_alpha * overall / (1.0 - circulant_alpha * block_decay**time_count)
    incoming = lead_power * start_value + offset
    exponents = jnp.arange(1, steps_local + 1, dtype=jnp.int32).astype(jnp.float32)
    powers = jnp.power(damping[None], exponents[:, None, None])
    return partial_value + powers * incoming[None]


def narrow_solve(planes, eigvec_x, eigval_x, shift_yz, time_count):
    steps_local, rows_x, size_y, size_z = planes.shape
    planes = planes.reshape(steps_local, rows_x, size_y * size_z)
    x_lines = lax.all_to_all(planes, "space", split_axis=2, concat_axis=1, tiled=True)
    x_lines = jnp.einsum("txm,xi->tim", x_lines, eigvec_x, precision=highest)
    shifts = eigval_x[:, None] + shift_yz.reshape(1, -1)
    x_lines = recurrence_solve(x_lines, shifts, time_count)
    x_lines = jnp.einsum("tim,xi->txm", x_lines, eigvec_x, precision=highest)
    planes = lax.all_to_all(x_lines, "space", split_axis=1, concat_axis=2, tiled=True)
    return planes.reshape(steps_local, rows_x, size_y, size_z)


def shards(residual_field, eigvec_x, eigvec_y, eigvec_z, eigval_x, eigval_y, eigval_z):
    steps_local, rows_x, size_y, size_z = residual_field.shape
    space_count = lax.axis_size("space")
    time_count = lax.axis_size("tm")
    planes = plane_transform(residual_field, eigvec_y.T, eigvec_z)
    band = size_y // space_count
    shift_y = lax.dynamic_slice_in_dim(eigval_y, lax.axis_index("space") * band, band, 0)
    shift_yz = shift_y[:, None] + eigval_z[None, :]
    if band % tile_rows == 0 and rows_x % tile_rows == 0:
        planes = exchange_solve(planes, eigvec_x, eigval_x, shift_yz, space_count, time_count)
    else:
        planes = narrow_solve(planes, eigvec_x, eigval_x, shift_yz, time_count)
    return plane_transform(planes, eigvec_y, eigvec_z.T)


def solution(mesh):
    placed = (P("tm", "space", None, None), P(), P(), P(), P(), P(), P())
    return jax.shard_map(
        shards, mesh=mesh, in_specs=placed, out_specs=P("tm", "space", None, None), check_vma=False
    )
```

profile of v0, /device:TPU:9, one launch (start us, length us, event | category | flops | bytes accessed | tf_op | source)
XLA Modules:
  0.0 820.4 jit_solution(10424495069124511891)
XLA Ops:
  0.0 0.7 dynamic_slice.3
  0.7 0.1 add.20
  0.8 1.3 broadcast_add_fusion.shift_ref
  2.1 1.6 copy.8
  3.7 0.0 copy-start
  3.7 0.0 copy-start.2
  3.7 44.5 %shard_map.73.in_ref = f32[16,16,128,128]{3,2,1,0:T(8,128)} custom-call(f32[16,16,128,128]{3,2,1,0:T(8,128)} %a_ref.1, f32[128,128]{1,0:T(8,128)} %bitcast.5, f32[128,128]{1,0:T(8,128)} %right_ref.1), custom_call_target="tpu_custom_call" | custom-call | tf_op jit(solution)/shard_map/pallas_call | solution.py:60
  48.2 0.0 copy-done
  48.2 0.7 copy.9
  48.9 0.0 copy-done.2
  48.9 0.7 broadcast_in_dim.2.ex_ref
  49.6 0.0 copy-start.1
  49.6 725.7 %shard_map.74.a_ref = f32[16,16,128,128]{3,2,1,0:T(8,128)} custom-call(f32[16,16,128,128]{3,2,1,0:T(8,128)} %shard_map.73.in_ref, f32[128,128]{1,0:T(8,128)} %bitcast.3, f32[128,128]{1,0:T(8,128)} %v_ref.1, f32[128,128]{1,0:T(8,128)} %broadcast_in_dim.2.ex_ref, f32[2,8,128]{2,1,0:T(8,128)} %broadcast_add_fusion.shift_ref), custom_call_target="tpu_custom_call" | custom-call | tf_op jit(solution)/shard_map/pallas_call | solution.py:248
  775.3 0.0 copy-done.1
  775.3 0.7 copy.10
  776.0 44.4 %shard_map.75 = f32[16,16,128,128]{3,2,1,0:T(8,128)} custom-call(f32[16,16,128,128]{3,2,1,0:T(8,128)} %shard_map.74.a_ref, f32[128,128]{1,0:T(8,128)} %left_ref.1, f32[128,128]{1,0:T(8,128)} %bitcast.4), custom_call_target="tpu_custom_call" | custom-call | tf_op jit(solution)/shard_map/pallas_call | solution.py:60
Async XLA Ops:
  3.7 44.5 %copy-start = (f32[128,128]{1,0:T(8,128)S(1)}, f32[128,128]{1,0:T(8,128)}, u32[]{:S(2)}) copy-start(f32[128,128]{1,0:T(8,128)} %v_ref.1) | copy-start | bytes 196612
  3.7 45.2 %copy-start.2 = (f32[128]{0:T(128)S(1)}, f32[128]{0:T(128)}, u32[]{:S(2)}) copy-start(f32[128]{0:T(128)} %param.11) | copy-start | bytes 1540
  49.6 725.7 %copy-start.1 = (f32[128,128]{1,0:T(8,128)S(1)}, f32[128,128]{1,0:T(8,128)}, u32[]{:S(2)}) copy-start(f32[128,128]{1,0:T(8,128)} %right_ref.1) | copy-start | bytes 196612
where the time goes:
time: 821 us; the launch traced here: 820 us
  Pallas kernels  815 us (99%)
    pallas_call x1, Pallas kernels, exchange_solve(): pl.pallas_call(functools.partial(exchange_kernel, space_count, time_count...  726 us
    pallas_call x2, Pallas kernels, plane_transform(): pl.pallas_call(plane_kernel, grid=(steps,), in_specs=[block, whole(left),...  88.9 us

commit v1 on v0

v1 whole, which is shorter than its diff:
```python
import functools
import jax
import jax.numpy as jnp
from jax import lax
from jax.experimental import pallas as pl
from jax.experimental.pallas import tpu as pltpu
from jax.sharding import PartitionSpec as P

highest = lax.Precision.HIGHEST
circulant_alpha = 0.01
tile_rows = 8


def halves(a):
    high = a.astype(jnp.bfloat16)
    return high, (a - high.astype(jnp.float32)).astype(jnp.bfloat16)


def stacked(matrix):
    return jnp.concatenate(halves(matrix), axis=0)


def left_product(left, a):
    rows, columns = left.shape[0] // 2, a.shape[1]
    r = jnp.dot(left, jnp.concatenate(halves(a), axis=1), preferred_element_type=jnp.float32)
    return (r[:rows, :columns] + r[rows:, :columns]) + (r[:rows, columns:] + r[rows:, columns:])


def right_product(a, right):
    columns = right.shape[1] // 2
    r = jnp.dot(jnp.concatenate(halves(a), axis=1), right, preferred_element_type=jnp.float32)
    return r[:, :columns] + r[:, columns:]


def power(a, n):
    result = None
    while n:
        if n & 1:
            result = a if result is None else result * a
        a, n = a * a, n >> 1
    return result


def plane_kernel(a_ref, left_ref, right_ref, o_ref):
    left = stacked(left_ref[...])
    right = jnp.concatenate(halves(right_ref[...]), axis=1)
    right = jnp.concatenate([right, right], axis=0)

    def one(x, carry):
        o_ref[0, x] = left_product(left, right_product(a_ref[0, x], right))
        return carry

    lax.fori_loop(0, a_ref.shape[1], one, 0, unroll=4)


def plane_transform(a, left, right):
    steps, rows, size_y, size_z = a.shape
    block = pl.BlockSpec((1, rows, size_y, size_z), lambda t: (t, 0, 0, 0))
    whole = lambda m: pl.BlockSpec(m.shape, lambda t: (0, 0))
    return pl.pallas_call(
        plane_kernel,
        grid=(steps,),
        in_specs=[block, whole(left), whole(right)],
        out_specs=block,
        out_shape=jax.ShapeDtypeStruct(a.shape, jnp.float32),
        compiler_params=pltpu.CompilerParams(vmem_limit_bytes=60 * 2**20),
    )(a, left, right)


def step_groups(steps):
    if steps < 8:
        return [(0, steps)]
    return [(0, 1), (1, 3), (4, steps - 4)]


def reversed_groups(groups):
    steps = sum(count for _, count in groups)
    return [(steps - start - count, count) for start, count in reversed(groups)]


def fused_kernel(
    space_count, time_count, chunks,
    in_ref, vx_ref, vy_ref, vz_ref, ex_ref, ey_ref, ez_ref, out_ref,
    send, recv, fins, entry, ex, shift,
    load_sem, own_in, own_out, go_send, go_recv, back_send, back_recv, st_send, st_recv,
):
    steps, rows, band_rows = recv.shape[2], recv.shape[3], recv.shape[4]
    size_x, size_z = fins.shape[3], fins.shape[4]
    size_y = vy_ref.shape[0]
    band = band_rows * chunks
    me = lax.axis_index("space")
    position = lax.axis_index("tm")
    small_first = step_groups(steps)
    whole = [(0, steps)]
    go_groups = [(c, *g) for c in range(chunks) for g in (small_first if c == 0 else whole)]
    back_groups = [
        (c, *g)
        for c in range(chunks)
        for g in (reversed_groups(small_first) if c == chunks - 1 else whole)
    ]

    def peer_of(k):
        return lax.rem(me + k, space_count)

    def timer_of(k):
        return lax.rem(position + k, time_count)

    def columns(owner, c):
        return pl.ds(pl.multiple_of(owner * band + c * band_rows, tile_rows), band_rows)

    def go(g, peer, slot):
        c, start, count = go_groups[g]
        return pltpu.make_async_remote_copy(
            src_ref=send.at[pl.ds(start, count), :, columns(peer, c), :],
            dst_ref=recv.at[c, slot, pl.ds(start, count)],
            send_sem=go_send.at[g, peer],
            recv_sem=go_recv.at[g, slot],
            device_id={"space": peer},
            device_id_type=pl.DeviceIdType.MESH,
        )

    def back(g, peer, slot):
        c, start, count = back_groups[g]
        return pltpu.make_async_remote_copy(
            src_ref=recv.at[c, peer, pl.ds(start, count)],
            dst_ref=out_ref.at[pl.ds(start, count), :, columns(slot, c), :],
            send_sem=back_send.at[g, peer],
            recv_sem=back_recv.at[g, slot],
            device_id={"space": peer},
            device_id_type=pl.DeviceIdType.MESH,
        )

    def final(c, peer, owner):
        return pltpu.make_async_remote_copy(
            src_ref=fins.at[c, owner],
            dst_ref=fins.at[c, owner],
            send_sem=st_send.at[c, peer],
            recv_sem=st_recv.at[c, owner],
            device_id={"tm": peer},
            device_id_type=pl.DeviceIdType.MESH,
        )

    def take_own(g):
        c, start, count = go_groups[g]
        return pltpu.make_async_copy(
            send.at[pl.ds(start, count), :, columns(me, c), :],
            recv.at[c, me, pl.ds(start, count)],
            own_in.at[g],
        )

    def give_own(g):
        c, start, count = back_groups[g]
        return pltpu.make_async_copy(
            recv.at[c, me, pl.ds(start, count)],
            out_ref.at[pl.ds(start, count), :, columns(me, c), :],
            own_out.at[g],
        )

    def load_step(t):
        return pltpu.make_async_copy(in_ref.at[t], send.at[t], load_sem.at[t])

    def start_load(t, carry):
        load_step(t).start()
        return carry

    lax.fori_loop(0, steps, start_load, 0)

    barrier = pltpu.get_barrier_semaphore()
    for k in range(1, space_count):
        pl.semaphore_signal(
            barrier, inc=1, device_id={"space": peer_of(k)}, device_id_type=pl.DeviceIdType.MESH
        )
    for k in range(1, time_count):
        pl.semaphore_signal(
            barrier, inc=1, device_id={"tm": timer_of(k)}, device_id_type=pl.DeviceIdType.MESH
        )

    middle = space_count // 2
    offsets = sorted(range(1, space_count), key=lambda k: abs(k - middle))

    def plane_loop(ref, start, count, left, right, arrived):
        def one_step(t, carry):
            arrived(t)

            def one(x, carry):
                ref[t, x] = left_product(left, right_product(ref[t, x], right))
                return carry

            return lax.fori_loop(0, rows, one, carry, unroll=4)

        lax.fori_loop(start, start + count, one_step, 0)

    def right_factor(matrix):
        both = jnp.concatenate(halves(matrix), axis=1)
        return jnp.concatenate([both, both], axis=0)

    left = stacked(vy_ref[...].T)
    right = right_factor(vz_ref[...])
    for g, (c, start, count) in enumerate(go_groups):
        if c == 0:
            plane_loop(send, start, count, left, right, lambda t: load_step(t).wait())
        if g == 0:
            pl.semaphore_wait(barrier, space_count + time_count - 2)
        for k in offsets:
            go(g, peer_of(k), me).start()
        take_own(g).start()

    ex[...] = jnp.broadcast_to(ex_ref[...], (size_z, size_x)).T
    shift[...] = jnp.broadcast_to(ey_ref[...], (size_z, size_y)).T + ez_ref[...]
    left = stacked(vx_ref[...].T)
    left_back = stacked(vx_ref[...])

    def load(c, t, j):
        parts = [
            recv.at[c, s, t].reshape(rows * band_rows, size_z)[pl.ds(j, rows, stride=band_rows), :]
            for s in range(space_count)
        ]
        return jnp.concatenate(parts, axis=0)

    def store(c, t, j, value):
        for s in range(space_count):
            view = recv.at[c, s, t].reshape(rows * band_rows, size_z)
            view[pl.ds(j, rows, stride=band_rows), :] = value[s * rows : (s + 1) * rows]

    def damping_of(c, j):
        row = shift[pl.ds(me * band + c * band_rows + j, 1), :]
        return 1.0 / (1.0 + (ex[...] + row))

    for c in range(chunks):
        for g, (of, start, count) in enumerate(go_groups):
            if of != c:
                continue
            for k in offsets:
                go(g, peer_of(k), peer_of(k)).wait_recv()
            take_own(g).wait()

            def forward_mode(j, carry, c=c, start=start, count=count):
                damping = damping_of(c, j)

                def forward(t, state):
                    state = damping * (state + left_product(left, load(c, t, j)))
                    store(c, t, j, state)
                    return state

                first = jnp.zeros_like(damping) if start == 0 else fins[c, position, j]
                fins[c, position, j] = lax.fori_loop(
                    start, start + count, forward, first, unroll=2 if count % 2 == 0 else 1
                )
                return carry

            lax.fori_loop(0, band_rows, forward_mode, 0)
        for k in range(1, time_count):
            final(c, timer_of(k), position).start()
        for k in range(1, time_count):
            final(c, timer_of(k), timer_of(k)).wait_recv()
        for g, (of, start, count) in enumerate(back_groups):
            if of != c:
                continue

            def inverse_mode(j, carry, c=c, start=start, count=count):
                damping = damping_of(c, j)
                if start == 0:
                    block_decay = power(damping, steps)
                    overall = fins[c, 0, j]
                    for p in range(1, time_count):
                        overall = block_decay * overall + fins[c, p, j]
                    incoming = (circulant_alpha * overall) / (
                        1.0 - circulant_alpha * power(block_decay, time_count)
                    )
                    for p in range(time_count - 1):
                        incoming = jnp.where(
                            p < position, block_decay * incoming + fins[c, p, j], incoming
                        )
                else:
                    incoming = entry[j]

                def inverse(t, incoming):
                    incoming = damping * incoming
                    store(c, t, j, left_product(left_back, load(c, t, j) + incoming))
                    return incoming

                entry[j] = lax.fori_loop(
                    start, start + count, inverse, incoming, unroll=2 if count % 2 == 0 else 1
                )
                return carry

            lax.fori_loop(0, band_rows, inverse_mode, 0)
            for k in offsets:
                back(g, peer_of(k), me).start()
            give_own(g).start()

    left = stacked(vy_ref[...])
    right = right_factor(vz_ref[...].T)
    for g, (c, start, count) in enumerate(back_groups):
        for k in offsets:
            back(g, peer_of(k), peer_of(k)).wait_recv()
        give_own(g).wait()
        if c == chunks - 1:
            plane_loop(out_ref, start, count, left, right, lambda t: None)

    for c in range(chunks):
        for k in range(1, time_count):
            final(c, timer_of(k), position).wait_send()
    for g in range(len(go_groups)):
        for k in offsets:
            go(g, peer_of(k), me).wait_send()
    for g in range(len(back_groups)):
        for k in offsets:
            back(g, peer_of(k), me).wait_send()


def chunk_count(band):
    return 2 if band % (2 * tile_rows) == 0 else 1


def fused_solve(field, eigvec_x, eigvec_y, eigvec_z, eigval_x, eigval_y, eigval_z):
    space_count = lax.axis_size("space")
    time_count = lax.axis_size("tm")
    steps, rows, size_y, size_z = field.shape
    band = size_y // space_count
    chunks = chunk_count(band)
    band_rows = band // chunks
    size_x = rows * space_count
    messages = chunks - 1 + len(step_groups(steps))
    vmem = pl.BlockSpec(memory_space=pltpu.VMEM)
    dma = pltpu.SemaphoreType.DMA
    f32 = jnp.float32
    return pl.pallas_call(
        functools.partial(fused_kernel, space_count, time_count, chunks),
        in_specs=[pl.BlockSpec(memory_space=pl.ANY)] + [vmem] * 6,
        out_specs=vmem,
        out_shape=pltpu.VMEM(field.shape, f32),
        scratch_shapes=[
            pltpu.VMEM(field.shape, f32),
            pltpu.VMEM((chunks, space_count, steps, rows, band_rows, size_z), f32),
            pltpu.VMEM((chunks, time_count, band_rows, size_x, size_z), f32),
            pltpu.VMEM((band_rows, size_x, size_z), f32),
            pltpu.VMEM((size_x, size_z), f32),
            pltpu.VMEM((size_y, size_z), f32),
            dma((steps,)),
            dma((messages,)),
            dma((messages,)),
            dma((messages, space_count)),
            dma((messages, space_count)),
            dma((messages, space_count)),
            dma((messages, space_count)),
            dma((chunks, time_count)),
            dma((chunks, time_count)),
        ],
        compiler_params=pltpu.CompilerParams(
            collective_id=0, has_side_effects=True, vmem_limit_bytes=44 * 2**20
        ),
    )(
        field,
        eigvec_x,
        eigvec_y,
        eigvec_z,
        eigval_x.reshape(1, -1),
        eigval_y.reshape(1, -1),
        eigval_z.reshape(1, -1),
    )


def entering(part, axis, combine, identity):
    place = lax.axis_index(axis)
    gathered = jax.tree.map(lambda a: lax.all_gather(a, axis), part)
    state = jax.tree.map(lambda a, e: jnp.zeros_like(a) + jnp.asarray(e, a.dtype), part, identity)

    def one(step, state):
        return combine(
            state, jax.tree.map(lambda a: lax.dynamic_index_in_dim(a, step, 0, False), gathered)
        )

    return lax.fori_loop(0, place, one, state)


def recurrence_solve(values, shifts, time_count):
    steps_local = values.shape[0]
    damping = 1.0 / (1.0 + shifts)

    def advance(running, step_row):
        running = damping * (running + step_row)
        return (running, running)

    final_state, partial_value = lax.scan(advance, jnp.zeros_like(shifts), values)
    block_decay = damping**steps_local
    position = lax.axis_index("tm")

    def compose(early_map, late_map):
        return (early_map[0] * late_map[0], late_map[0] * early_map[1] + late_map[1])

    lead_power, offset = entering(
        (block_decay, final_state), "tm", compose, (jnp.ones_like(shifts), jnp.zeros_like(shifts))
    )
    tail_power = jnp.power(block_decay, (time_count - 1 - position).astype(jnp.float32))
    overall = lax.psum(tail_power * final_state, "tm")
    start_value = circulant_alpha * overall / (1.0 - circulant_alpha * block_decay**time_count)
    incoming = lead_power * start_value + offset
    exponents = jnp.arange(1, steps_local + 1, dtype=jnp.int32).astype(jnp.float32)
    powers = jnp.power(damping[None], exponents[:, None, None])
    return partial_value + powers * incoming[None]


def narrow_solve(planes, eigvec_x, eigval_x, shift_yz, time_count):
    steps_local, rows_x, size_y, size_z = planes.shape
    planes = planes.reshape(steps_local, rows_x, size_y * size_z)
    x_lines = lax.all_to_all(planes, "space", split_axis=2, concat_axis=1, tiled=True)
    x_lines = jnp.einsum("txm,xi->tim", x_lines, eigvec_x, precision=highest)
    shifts = eigval_x[:, None] + shift_yz.reshape(1, -1)
    x_lines = recurrence_solve(x_lines, shifts, time_count)
    x_lines = jnp.einsum("tim,xi->txm", x_lines, eigvec_x, precision=highest)
    planes = lax.all_to_all(x_lines, "space", split_axis=1, concat_axis=2, tiled=True)
    return planes.reshape(steps_local, rows_x, size_y, size_z)


def fits(field, space_count, time_count):
    steps, rows, size_y, size_z = field.shape
    band = size_y // space_count
    if band % tile_rows or rows % tile_rows:
        return False
    states = (time_count + 1) * band * rows * space_count * size_z
    return 4 * (3 * field.size + states) < 60 * 2**20


def shards(residual_field, eigvec_x, eigvec_y, eigvec_z, eigval_x, eigval_y, eigval_z):
    size_y = residual_field.shape[2]
    space_count = lax.axis_size("space")
    time_count = lax.axis_size("tm")
    if fits(residual_field, space_count, time_count):
        return fused_solve(
            residual_field, eigvec_x, eigvec_y, eigvec_z, eigval_x, eigval_y, eigval_z
        )
    planes = plane_transform(residual_field, eigvec_y.T, eigvec_z)
    band = size_y // space_count
    shift_y = lax.dynamic_slice_in_dim(eigval_y, lax.axis_index("space") * band, band, 0)
    shift_yz = shift_y[:, None] + eigval_z[None, :]
    planes = narrow_solve(planes, eigvec_x, eigval_x, shift_yz, time_count)
    return plane_transform(planes, eigvec_y, eigvec_z.T)


def solution(mesh):
    placed = (P("tm", "space", None, None), P(), P(), P(), P(), P(), P())
    return jax.shard_map(
        shards, mesh=mesh, in_specs=placed, out_specs=P("tm", "space", None, None), check_vma=False
    )
```

time: 821 us -> 754 us (0.918)
  Pallas kernels: 815 us -> 748 us
    pallas_call x3 -> x1, Pallas kernels: 815 us -> 748 us  [fused_solve(): pl.pallas_call(functools.partial(fused_kernel, space_count, time_count, c...]
where the time goes in v1:
time: 754 us
  Pallas kernels  748 us (99%)
    pallas_call x1, Pallas kernels, fused_solve(): pl.pallas_call(functools.partial(fused_kernel, space_count, time_count, c...  748 us

profile of v1, /device:TPU:9, one launch (start us, length us, event | category | flops | bytes accessed | tf_op | source)
XLA Modules:
  0.0 754.3 jit_solution(11285682858433264312)
XLA Ops:
  0.0 748.2 %shard_map.73 = f32[16,16,128,128]{3,2,1,0:T(8,128)S(1)} custom-call(f32[16,16,128,128]{3,2,1,0:T(8,128)} %in_ref.1, f32[128,128]{1,0:T(8,128)} %vx_ref.1, f32[128,128]{1,0:T(8,128)} %vy_ref.1, f32[128,128]{1,0:T(8,128)} %vz_ref.1, f32[1,128]{1,0:T(1,128)} %bitcast.3, f32[1,128]{1,0:T(1,128)} %bitcast.4, f32[1,128]{1,0:T(1,128)} %bitcast.5), custom_call_target="tpu_custom_call" | custom-call | tf_op jit(solution)/shard_map/pallas_call | solution.py:328
  748.2 6.2 copy.9

commit v2 on v1

v2 whole, which is shorter than its diff:
```python
import functools
import jax
import jax.numpy as jnp
from jax import lax
from jax.experimental import pallas as pl
from jax.experimental.pallas import tpu as pltpu
from jax.sharding import PartitionSpec as P

highest = lax.Precision.HIGHEST
circulant_alpha = 0.01
tile_rows = 8


def halves(a):
    high = a.astype(jnp.bfloat16)
    return high, (a - high.astype(jnp.float32)).astype(jnp.bfloat16)


def stacked(matrix):
    return jnp.concatenate(halves(matrix), axis=0)


def left_product(left, a):
    rows, columns = left.shape[0] // 2, a.shape[1]
    r = jnp.dot(left, jnp.concatenate(halves(a), axis=1), preferred_element_type=jnp.float32)
    return (r[:rows, :columns] + r[rows:, :columns]) + (r[:rows, columns:] + r[rows:, columns:])


def right_product(a, right):
    columns = right.shape[1] // 2
    r = jnp.dot(jnp.concatenate(halves(a), axis=1), right, preferred_element_type=jnp.float32)
    return r[:, :columns] + r[:, columns:]


def power(a, n):
    result = None
    while n:
        if n & 1:
            result = a if result is None else result * a
        a, n = a * a, n >> 1
    return result


def plane_kernel(a_ref, left_ref, right_ref, o_ref):
    left = stacked(left_ref[...])
    right = jnp.concatenate(halves(right_ref[...]), axis=1)
    right = jnp.concatenate([right, right], axis=0)

    def one(x, carry):
        o_ref[0, x] = left_product(left, right_product(a_ref[0, x], right))
        return carry

    lax.fori_loop(0, a_ref.shape[1], one, 0, unroll=4)


def plane_transform(a, left, right):
    steps, rows, size_y, size_z = a.shape
    block = pl.BlockSpec((1, rows, size_y, size_z), lambda t: (t, 0, 0, 0))
    whole = lambda m: pl.BlockSpec(m.shape, lambda t: (0, 0))
    return pl.pallas_call(
        plane_kernel,
        grid=(steps,),
        in_specs=[block, whole(left), whole(right)],
        out_specs=block,
        out_shape=jax.ShapeDtypeStruct(a.shape, jnp.float32),
        compiler_params=pltpu.CompilerParams(vmem_limit_bytes=60 * 2**20),
    )(a, left, right)


def spans(sizes):
    starts = [sum(sizes[:i]) for i in range(len(sizes))]
    return list(zip(starts, sizes))


def growing(total):
    if total % 256:
        return [total]
    return [total // 64, 3 * total // 64, 12 * total // 64, 48 * total // 64]


def shrinking(total):
    sizes = []
    while total > 4 and total % 8 == 0:
        total //= 2
        sizes.append(total)
    return sizes + [total]


def messages(chunks, total):
    outward = [(0, *s) for s in spans(growing(total))]
    outward += [(c, 0, total) for c in range(1, chunks)]
    homeward = [(c, 0, total) for c in range(chunks - 1)]
    homeward += [(chunks - 1, *s) for s in spans(shrinking(total))]
    return outward, homeward


def fused_kernel(
    space_count, time_count, chunks, rows,
    in_ref, vx_ref, vy_ref, vz_ref, ex_ref, ey_ref, ez_ref, out_ref,
    send, recv, fins, matrices, ex, shift,
    load_sem, matrix_sem, own_in, own_out,
    go_send, go_recv, back_send, back_recv, st_send, st_recv,
):
    total, band_rows = recv.shape[2], recv.shape[3]
    size_x, size_z = fins.shape[3], fins.shape[4]
    size_y = vy_ref.shape[0]
    steps = total // rows
    band = band_rows * chunks
    me = lax.axis_index("space")
    position = lax.axis_index("tm")
    outward, homeward = messages(chunks, total)
    middle = space_count // 2
    offsets = sorted(range(1, space_count), key=lambda k: abs(k - middle))

    def peer_of(k):
        return lax.rem(me + k, space_count)

    def timer_of(k):
        return lax.rem(position + k, time_count)

    def columns(owner, c):
        return pl.ds(pl.multiple_of(owner * band + c * band_rows, tile_rows), band_rows)

    def go(g, peer, slot):
        c, start, count = outward[g]
        return pltpu.make_async_remote_copy(
            src_ref=send.at[pl.ds(start, count), columns(peer, c), :],
            dst_ref=recv.at[c, slot, pl.ds(start, count)],
            send_sem=go_send.at[g, peer],
            recv_sem=go_recv.at[g, slot],
            device_id={"space": peer},
            device_id_type=pl.DeviceIdType.MESH,
        )

    def back(g, peer, slot):
        c, start, count = homeward[g]
        return pltpu.make_async_remote_copy(
            src_ref=recv.at[c, peer, pl.ds(start, count)],
            dst_ref=out_ref.at[pl.ds(start, count), columns(slot, c), :],
            send_sem=back_send.at[g, peer],
            recv_sem=back_recv.at[g, slot],
            device_id={"space": peer},
            device_id_type=pl.DeviceIdType.MESH,
        )

    def final(c, peer, owner):
        return pltpu.make_async_remote_copy(
            src_ref=fins.at[c, owner],
            dst_ref=fins.at[c, owner],
            send_sem=st_send.at[c, peer],
            recv_sem=st_recv.at[c, owner],
            device_id={"tm": peer},
            device_id_type=pl.DeviceIdType.MESH,
        )

    def take_own(g):
        c, start, count = outward[g]
        return pltpu.make_async_copy(
            send.at[pl.ds(start, count), columns(me, c), :],
            recv.at[c, me, pl.ds(start, count)],
            own_in.at[g],
        )

    def give_own(g):
        c, start, count = homeward[g]
        return pltpu.make_async_copy(
            recv.at[c, me, pl.ds(start, count)],
            out_ref.at[pl.ds(start, count), columns(me, c), :],
            own_out.at[g],
        )

    loads = [
        pltpu.make_async_copy(
            in_ref.at[pl.ds(start, count)], send.at[pl.ds(start, count)], load_sem.at[g]
        )
        for g, (start, count) in enumerate(spans(growing(total)))
    ]
    fetches = [
        pltpu.make_async_copy(ref, matrices.at[i], matrix_sem.at[i])
        for i, ref in enumerate((vz_ref, vy_ref, vx_ref))
    ]
    barrier = pltpu.get_barrier_semaphore()
    for k in range(1, space_count):
        pl.semaphore_signal(
            barrier, inc=1, device_id={"space": peer_of(k)}, device_id_type=pl.DeviceIdType.MESH
        )
    for k in range(1, time_count):
        pl.semaphore_signal(
            barrier, inc=1, device_id={"tm": timer_of(k)}, device_id_type=pl.DeviceIdType.MESH
        )
    for copy in fetches[:2] + loads + fetches[2:]:
        copy.start()

    def transform_planes(ref, start, count, left, right):
        def one(u, carry):
            ref[u] = left_product(left, right_product(ref[u], right))
            return carry

        lax.fori_loop(start, start + count, one, 0, unroll=4)

    def right_factor(matrix):
        both = jnp.concatenate(halves(matrix), axis=1)
        return jnp.concatenate([both, both], axis=0)

    fetches[0].wait()
    right = right_factor(matrices[0])
    fetches[1].wait()
    left = stacked(matrices[1].T)
    for g, (c, start, count) in enumerate(outward):
        if c == 0:
            loads[g].wait()
            transform_planes(send, start, count, left, right)
        if g == 0:
            pl.semaphore_wait(barrier, space_count + time_count - 2)
        for k in offsets:
            go(g, peer_of(k), me).start()
        take_own(g).start()

    ex[...] = jnp.broadcast_to(ex_ref[...], (size_z, size_x)).T
    shift[...] = jnp.broadcast_to(ey_ref[...], (size_z, size_y)).T + ez_ref[...]
    fetches[2].wait()
    left = stacked(matrices[2].T)
    left_back = stacked(matrices[2])

    def view(c, s, t):
        return recv.at[c, s, pl.ds(t * rows, rows)].reshape(rows * band_rows, size_z)

    def load(c, t, j):
        parts = [view(c, s, t)[pl.ds(j, rows, stride=band_rows), :] for s in range(space_count)]
        return jnp.concatenate(parts, axis=0)

    def store(c, t, j, value):
        for s in range(space_count):
            view(c, s, t)[pl.ds(j, rows, stride=band_rows), :] = value[s * rows : (s + 1) * rows]

    def damping_of(c, j):
        row = shift[pl.ds(me * band + c * band_rows + j, 1), :]
        return 1.0 / (1.0 + (ex[...] + row))

    for c in range(chunks):
        for g in range(len(outward)):
            if outward[g][0] == c:
                for k in offsets:
                    go(g, peer_of(k), peer_of(k)).wait_recv()
                take_own(g).wait()

        def forward_mode(j, carry, c=c):
            damping = damping_of(c, j)

            def forward(t, state):
                state = damping * (state + left_product(left, load(c, t, j)))
                store(c, t, j, state)
                return state

            fins[c, position, j] = lax.fori_loop(
                0, steps, forward, jnp.zeros_like(damping), unroll=2
            )
            return carry

        lax.fori_loop(0, band_rows, forward_mode, 0)
        for k in range(1, time_count):
            final(c, timer_of(k), position).start()
        for k in range(1, time_count):
            final(c, timer_of(k), timer_of(k)).wait_recv()

        def inverse_mode(j, carry, c=c):
            damping = damping_of(c, j)
            block_decay = power(damping, steps)
            overall = fins[c, 0, j]
            for p in range(1, time_count):
                overall = block_decay * overall + fins[c, p, j]
            incoming = (circulant_alpha * overall) / (
                1.0 - circulant_alpha * power(block_decay, time_count)
            )
            for p in range(time_count - 1):
                incoming = jnp.where(
                    p < position, block_decay * incoming + fins[c, p, j], incoming
                )

            def inverse(t, incoming):
                incoming = damping * incoming
                store(c, t, j, left_product(left_back, load(c, t, j) + incoming))
                return incoming

            lax.fori_loop(0, steps, inverse, incoming, unroll=2)
            return carry

        lax.fori_loop(0, band_rows, inverse_mode, 0)
        for g in range(len(homeward)):
            if homeward[g][0] == c:
                for k in offsets:
                    back(g, peer_of(k), me).start()
                give_own(g).start()

    left = stacked(matrices[1])
    right = right_factor(matrices[0].T)
    for g, (c, start, count) in enumerate(homeward):
        for k in offsets:
            back(g, peer_of(k), peer_of(k)).wait_recv()
        give_own(g).wait()
        if c == chunks - 1:
            transform_planes(out_ref, start, count, left, right)

    for c in range(chunks):
        for k in range(1, time_count):
            final(c, timer_of(k), position).wait_send()
    for g in range(len(outward)):
        for k in offsets:
            go(g, peer_of(k), me).wait_send()
    for g in range(len(homeward)):
        for k in offsets:
            back(g, peer_of(k), me).wait_send()


def fused_solve(field, eigvec_x, eigvec_y, eigvec_z, eigval_x, eigval_y, eigval_z):
    space_count = lax.axis_size("space")
    time_count = lax.axis_size("tm")
    steps, rows, size_y, size_z = field.shape
    planes = field.reshape(steps * rows, size_y, size_z)
    band = size_y // space_count
    chunks = 2 if band % (2 * tile_rows) == 0 else 1
    band_rows = band // chunks
    size_x = rows * space_count
    outward, homeward = messages(chunks, steps * rows)
    vmem = pl.BlockSpec(memory_space=pltpu.VMEM)
    hbm = pl.BlockSpec(memory_space=pl.ANY)
    dma = pltpu.SemaphoreType.DMA
    f32 = jnp.float32
    update = pl.pallas_call(
        functools.partial(fused_kernel, space_count, time_count, chunks, rows),
        in_specs=[hbm] * 4 + [vmem] * 3,
        out_specs=vmem,
        out_shape=pltpu.VMEM(planes.shape, f32),
        scratch_shapes=[
            pltpu.VMEM(planes.shape, f32),
            pltpu.VMEM((chunks, space_count, steps * rows, band_rows, size_z), f32),
            pltpu.VMEM((chunks, time_count, band_rows, size_x, size_z), f32),
            pltpu.VMEM((3, size_y, size_z), f32),
            pltpu.VMEM((size_x, size_z), f32),
            pltpu.VMEM((size_y, size_z), f32),
            dma((len(growing(steps * rows)),)),
            dma((3,)),
            dma((len(outward),)),
            dma((len(homeward),)),
            dma((len(outward), space_count)),
            dma((len(outward), space_count)),
            dma((len(homeward), space_count)),
            dma((len(homeward), space_count)),
            dma((chunks, time_count)),
            dma((chunks, time_count)),
        ],
        compiler_params=pltpu.CompilerParams(
            collective_id=0, has_side_effects=True, vmem_limit_bytes=44 * 2**20
        ),
    )(
        planes,
        eigvec_x,
        eigvec_y,
        eigvec_z,
        eigval_x.reshape(1, -1),
        eigval_y.reshape(1, -1),
        eigval_z.reshape(1, -1),
    )
    return update.reshape(field.shape)


def entering(part, axis, combine, identity):
    place = lax.axis_index(axis)
    gathered = jax.tree.map(lambda a: lax.all_gather(a, axis), part)
    state = jax.tree.map(lambda a, e: jnp.zeros_like(a) + jnp.asarray(e, a.dtype), part, identity)

    def one(step, state):
        return combine(
            state, jax.tree.map(lambda a: lax.dynamic_index_in_dim(a, step, 0, False), gathered)
        )

    return lax.fori_loop(0, place, one, state)


def recurrence_solve(values, shifts, time_count):
    steps_local = values.shape[0]
    damping = 1.0 / (1.0 + shifts)

    def advance(running, step_row):
        running = damping * (running + step_row)
        return (running, running)

    final_state, partial_value = lax.scan(advance, jnp.zeros_like(shifts), values)
    block_decay = damping**steps_local
    position = lax.axis_index("tm")

    def compose(early_map, late_map):
        return (early_map[0] * late_map[0], late_map[0] * early_map[1] + late_map[1])

    lead_power, offset = entering(
        (block_decay, final_state), "tm", compose, (jnp.ones_like(shifts), jnp.zeros_like(shifts))
    )
    tail_power = jnp.power(block_decay, (time_count - 1 - position).astype(jnp.float32))
    overall = lax.psum(tail_power * final_state, "tm")
    start_value = circulant_alpha * overall / (1.0 - circulant_alpha * block_decay**time_count)
    incoming = lead_power * start_value + offset
    exponents = jnp.arange(1, steps_local + 1, dtype=jnp.int32).astype(jnp.float32)
    powers = jnp.power(damping[None], exponents[:, None, None])
    return partial_value + powers * incoming[None]


def narrow_solve(planes, eigvec_x, eigval_x, shift_yz, time_count):
    steps_local, rows_x, size_y, size_z = planes.shape
    planes = planes.reshape(steps_local, rows_x, size_y * size_z)
    x_lines = lax.all_to_all(planes, "space", split_axis=2, concat_axis=1, tiled=True)
    x_lines = jnp.einsum("txm,xi->tim", x_lines, eigvec_x, precision=highest)
    shifts = eigval_x[:, None] + shift_yz.reshape(1, -1)
    x_lines = recurrence_solve(x_lines, shifts, time_count)
    x_lines = jnp.einsum("tim,xi->txm", x_lines, eigvec_x, precision=highest)
    planes = lax.all_to_all(x_lines, "space", split_axis=1, concat_axis=2, tiled=True)
    return planes.reshape(steps_local, rows_x, size_y, size_z)


def fits(field, space_count, time_count):
    steps, rows, size_y, size_z = field.shape
    band = size_y // space_count
    if band % tile_rows or rows % tile_rows or not rows * space_count == size_y == size_z:
        return False
    states = (time_count + 1) * band * rows * space_count * size_z
    return 4 * (3 * field.size + states) < 60 * 2**20


def shards(residual_field, eigvec_x, eigvec_y, eigvec_z, eigval_x, eigval_y, eigval_z):
    size_y = residual_field.shape[2]
    space_count = lax.axis_size("space")
    time_count = lax.axis_size("tm")
    if fits(residual_field, space_count, time_count):
        return fused_solve(
            residual_field, eigvec_x, eigvec_y, eigvec_z, eigval_x, eigval_y, eigval_z
        )
    planes = plane_transform(residual_field, eigvec_y.T, eigvec_z)
    band = size_y // space_count
    shift_y = lax.dynamic_slice_in_dim(eigval_y, lax.axis_index("space") * band, band, 0)
    shift_yz = shift_y[:, None] + eigval_z[None, :]
    planes = narrow_solve(planes, eigvec_x, eigval_x, shift_yz, time_count)
    return plane_transform(planes, eigvec_y, eigvec_z.T)


def solution(mesh):
    placed = (P("tm", "space", None, None), P(), P(), P(), P(), P(), P())
    return jax.shard_map(
        shards, mesh=mesh, in_specs=placed, out_specs=P("tm", "space", None, None), check_vma=False
    )
```

time: 754 us -> 736 us (0.976)
  Pallas kernels: 748 us -> 728 us
    pallas_call x1, Pallas kernels: 748 us -> 728 us  [fused_solve(): pl.pallas_call(functools.partial(fused_kernel, space_count, time_count, c...]
where the time goes in v2:
time: 736 us; the launch traced here: 734 us
  Pallas kernels  728 us (99%)
    pallas_call x1, Pallas kernels, fused_solve(): pl.pallas_call(functools.partial(fused_kernel, space_count, time_count, c...  728 us

profile of v2, /device:TPU:9, one launch (start us, length us, event | category | flops | bytes accessed | tf_op | source)
XLA Modules:
  0.0 734.1 jit_solution(2068001578355346890)
XLA Ops:
  0.0 727.9 %shard_map.73 = f32[256,128,128]{2,1,0:T(8,128)S(1)} custom-call(f32[256,128,128]{2,1,0:T(8,128)} %bitcast.6, f32[128,128]{1,0:T(8,128)} %vx_ref.1, f32[128,128]{1,0:T(8,128)} %vy_ref.1, f32[128,128]{1,0:T(8,128)} %vz_ref.1, f32[1,128]{1,0:T(1,128)} %bitcast.7, f32[1,128]{1,0:T(1,128)} %bitcast.8, f32[1,128]{1,0:T(1,128)} %bitcast.9), custom_call_target="tpu_custom_call" | custom-call | tf_op jit(solution)/shard_map/pallas_call | solution.py:329
  728.0 6.2 copy.9

commit v3 on v2

--- a/solution.py
+++ b/solution.py
@@ -16,14 +16,19 @@
     return high, (a - high.astype(jnp.float32)).astype(jnp.bfloat16)
 
 
-def stacked(matrix):
-    return jnp.concatenate(halves(matrix), axis=0)
+def left_factor(matrix):
+    return jnp.concatenate(halves(matrix), axis=1)
+
+
+def right_factor(matrix):
+    both = jnp.concatenate(halves(matrix), axis=1)
+    return jnp.concatenate([both, both], axis=0)
 
 
 def left_product(left, a):
-    rows, columns = left.shape[0] // 2, a.shape[1]
-    r = jnp.dot(left, jnp.concatenate(halves(a), axis=1), preferred_element_type=jnp.float32)
-    return (r[:rows, :columns] + r[rows:, :columns]) + (r[:rows, columns:] + r[rows:, columns:])
+    columns = a.shape[1]
+    r = jnp.dot(left, right_factor(a), preferred_element_type=jnp.float32)
+    return r[:, :columns] + r[:, columns:]
 
 
 def right_product(a, right):
@@ -42,9 +47,8 @@
 
 
 def plane_kernel(a_ref, left_ref, right_ref, o_ref):
-    left = stacked(left_ref[...])
-    right = jnp.concatenate(halves(right_ref[...]), axis=1)
-    right = jnp.concatenate([right, right], axis=0)
+    left = left_factor(left_ref[...])
+    right = right_factor(right_ref[...])
 
     def one(x, carry):
         o_ref[0, x] = left_product(left, right_product(a_ref[0, x], right))
@@ -75,15 +79,13 @@
 def growing(total):
     if total % 256:
         return [total]
-    return [total // 64, 3 * total // 64, 12 * total // 64, 48 * total // 64]
+    return [total // 256 * share for share in (8, 56, 192)]
 
 
 def shrinking(total):
-    sizes = []
-    while total > 4 and total % 8 == 0:
-        total //= 2
-        sizes.append(total)
-    return sizes + [total]
+    if total % 256:
+        return [total]
+    return [total // 256 * share for share in (160, 64, 24, 8)]
 
 
 def messages(chunks, total):
@@ -97,8 +99,8 @@
 def fused_kernel(
     space_count, time_count, chunks, rows,
     in_ref, vx_ref, vy_ref, vz_ref, ex_ref, ey_ref, ez_ref, out_ref,
-    send, recv, fins, matrices, ex, shift,
-    load_sem, matrix_sem, own_in, own_out,
+    send, recv, fins, matrices, values, ex, shift,
+    load_sem, matrix_sem, value_sem, own_in, own_out,
     go_send, go_recv, back_send, back_recv, st_send, st_recv,
 ):
     total, band_rows = recv.shape[2], recv.shape[3]
@@ -179,6 +181,10 @@
         pltpu.make_async_copy(ref, matrices.at[i], matrix_sem.at[i])
         for i, ref in enumerate((vz_ref, vy_ref, vx_ref))
     ]
+    fetches += [
+        pltpu.make_async_copy(ref, values.at[i], value_sem.at[i])
+        for i, ref in enumerate((ex_ref, ey_ref, ez_ref))
+    ]
     barrier = pltpu.get_barrier_semaphore()
     for k in range(1, space_count):
         pl.semaphore_signal(
@@ -196,16 +202,12 @@
             ref[u] = left_product(left, right_product(ref[u], right))
             return carry
 
-        lax.fori_loop(start, start + count, one, 0, unroll=4)
-
-    def right_factor(matrix):
-        both = jnp.concatenate(halves(matrix), axis=1)
-        return jnp.concatenate([both, both], axis=0)
+        lax.fori_loop(start, start + count, one, 0, unroll=8 if count % 8 == 0 else 1)
 
     fetches[0].wait()
     right = right_factor(matrices[0])
     fetches[1].wait()
-    left = stacked(matrices[1].T)
+    left = left_factor(matrices[1].T)
     for g, (c, start, count) in enumerate(outward):
         if c == 0:
             loads[g].wait()
@@ -216,11 +218,12 @@
             go(g, peer_of(k), me).start()
         take_own(g).start()
 
-    ex[...] = jnp.broadcast_to(ex_ref[...], (size_z, size_x)).T
-    shift[...] = jnp.broadcast_to(ey_ref[...], (size_z, size_y)).T + ez_ref[...]
-    fetches[2].wait()
-    left = stacked(matrices[2].T)
-    left_back = stacked(matrices[2])
+    for copy in fetches[2:]:
+        copy.wait()
+    ex[...] = jnp.broadcast_to(values[0], (size_z, size_x)).T
+    shift[...] = jnp.broadcast_to(values[1], (size_z, size_y)).T + values[2]
+    left = left_factor(matrices[2].T)
+    left_back = left_factor(matrices[2])
 
     def view(c, s, t):
         return recv.at[c, s, pl.ds(t * rows, rows)].reshape(rows * band_rows, size_z)
@@ -292,7 +295,7 @@
                     back(g, peer_of(k), me).start()
                 give_own(g).start()
 
-    left = stacked(matrices[1])
+    left = left_factor(matrices[1])
     right = right_factor(matrices[0].T)
     for g, (c, start, count) in enumerate(homeward):
         for k in offsets:
@@ -328,7 +331,7 @@
     f32 = jnp.float32
     update = pl.pallas_call(
         functools.partial(fused_kernel, space_count, time_count, chunks, rows),
-        in_specs=[hbm] * 4 + [vmem] * 3,
+        in_specs=[hbm] * 7,
         out_specs=vmem,
         out_shape=pltpu.VMEM(planes.shape, f32),
         scratch_shapes=[
@@ -336,9 +339,11 @@
             pltpu.VMEM((chunks, space_count, steps * rows, band_rows, size_z), f32),
             pltpu.VMEM((chunks, time_count, band_rows, size_x, size_z), f32),
             pltpu.VMEM((3, size_y, size_z), f32),
+            pltpu.VMEM((3, 1, size_z), f32),
             pltpu.VMEM((size_x, size_z), f32),
             pltpu.VMEM((size_y, size_z), f32),
             dma((len(growing(steps * rows)),)),
+            dma((3,)),
             dma((3,)),
             dma((len(outward),)),
             dma((len(homeward),)),

time: 736 us -> 734 us (level)
  no operation moved by 1% of the time
where the time goes in v3:
time: 734 us; the launch traced here: 732 us
  Pallas kernels  726 us (99%)
    pallas_call x1, Pallas kernels, fused_solve(): pl.pallas_call(functools.partial(fused_kernel, space_count, time_count, c...  726 us

profile of v3, /device:TPU:9, one launch (start us, length us, event | category | flops | bytes accessed | tf_op | source)
XLA Modules:
  0.0 732.5 jit_solution(8822986419938739707)
XLA Ops:
  0.0 726.3 %shard_map.73 = f32[256,128,128]{2,1,0:T(8,128)S(1)} custom-call(f32[256,128,128]{2,1,0:T(8,128)} %bitcast.6, f32[128,128]{1,0:T(8,128)} %vx_ref.1, f32[128,128]{1,0:T(8,128)} %vy_ref.1, f32[128,128]{1,0:T(8,128)} %vz_ref.1, f32[1,128]{1,0:T(1,128)} %bitcast.7, f32[1,128]{1,0:T(1,128)} %bitcast.8, f32[1,128]{1,0:T(1,128)} %bitcast.9), custom_call_target="tpu_custom_call" | custom-call | tf_op jit(solution)/shard_map/pallas_call | solution.py:332
  726.3 6.2 copy.9

commit v4 on v3

--- a/solution.py
+++ b/solution.py
@@ -85,7 +85,15 @@
 def shrinking(total):
     if total % 256:
         return [total]
-    return [total // 256 * share for share in (160, 64, 24, 8)]
+    return [total // 256 * share for share in (160, 64, 16, 16)]
+
+
+def transform_planes(source, target, start, count, left, right, shift=0):
+    def one(u, carry):
+        target[u - shift] = left_product(left, right_product(source[u], right))
+        return carry
+
+    lax.fori_loop(start, start + count, one, 0, unroll=8 if count % 8 == 0 else 1)
 
 
 def messages(chunks, total):
@@ -197,13 +205,6 @@
     for copy in fetches[:2] + loads + fetches[2:]:
         copy.start()
 
-    def transform_planes(ref, start, count, left, right):
-        def one(u, carry):
-            ref[u] = left_product(left, right_product(ref[u], right))
-            return carry
-
-        lax.fori_loop(start, start + count, one, 0, unroll=8 if count % 8 == 0 else 1)
-
     fetches[0].wait()
     right = right_factor(matrices[0])
     fetches[1].wait()
@@ -211,7 +212,7 @@
     for g, (c, start, count) in enumerate(outward):
         if c == 0:
             loads[g].wait()
-            transform_planes(send, start, count, left, right)
+            transform_planes(send, send, start, count, left, right)
         if g == 0:
             pl.semaphore_wait(barrier, space_count + time_count - 2)
         for k in offsets:
@@ -301,8 +302,8 @@
         for k in offsets:
             back(g, peer_of(k), peer_of(k)).wait_recv()
         give_own(g).wait()
-        if c == chunks - 1:
-            transform_planes(out_ref, start, count, left, right)
+        if c == chunks - 1 and g < len(homeward) - 1:
+            transform_planes(out_ref, out_ref, start, count, left, right)
 
     for c in range(chunks):
         for k in range(1, time_count):
@@ -313,6 +314,46 @@
     for g in range(len(homeward)):
         for k in offsets:
             back(g, peer_of(k), me).wait_send()
+
+
+def closing_kernel(in_ref, left_ref, right_ref, out_ref, last, sems):
+    held = last.shape[0]
+    done = in_ref.shape[0] - held
+    pieces = sems.shape[0] - 1
+    piece = done // pieces
+    copies = [
+        pltpu.make_async_copy(
+            in_ref.at[pl.ds(i * piece, piece)], out_ref.at[pl.ds(i * piece, piece)], sems.at[i]
+        )
+        for i in range(pieces)
+    ]
+    for copy in copies:
+        copy.start()
+    left = left_factor(left_ref[...])
+    right = right_factor(right_ref[...].T)
+    transform_planes(in_ref, last, done, held, left, right, shift=done)
+    copies.append(pltpu.make_async_copy(last, out_ref.at[pl.ds(done, held)], sems.at[pieces]))
+    copies[-1].start()
+    for copy in copies:
+        copy.wait()
+
+
+def close(planes, left, right):
+    vmem = pl.BlockSpec(memory_space=pltpu.VMEM)
+    held = shrinking(planes.shape[0])[-1]
+    done = planes.shape[0] - held
+    pieces = 6 if done % 6 == 0 else 1
+    return pl.pallas_call(
+        closing_kernel,
+        in_specs=[vmem] * 3,
+        out_specs=pl.BlockSpec(memory_space=pltpu.HBM),
+        out_shape=jax.ShapeDtypeStruct(planes.shape, jnp.float32),
+        scratch_shapes=[
+            pltpu.VMEM((held, *planes.shape[1:]), jnp.float32),
+            pltpu.SemaphoreType.DMA((pieces + 1,)),
+        ],
+        compiler_params=pltpu.CompilerParams(vmem_limit_bytes=24 * 2**20),
+    )(planes, left, right)
 
 
 def fused_solve(field, eigvec_x, eigvec_y, eigvec_z, eigval_x, eigval_y, eigval_z):
@@ -366,7 +407,7 @@
         eigval_y.reshape(1, -1),
         eigval_z.reshape(1, -1),
     )
-    return update.reshape(field.shape)
+    return close(update, eigvec_y, eigvec_z).reshape(field.shape)
 
 
 def entering(part, axis, combine, identity):
@@ -424,7 +465,7 @@
 def fits(field, space_count, time_count):
     steps, rows, size_y, size_z = field.shape
     band = size_y // space_count
-    if band % tile_rows or rows % tile_rows or not rows * space_count == size_y == size_z:
+    if band % tile_rows or rows % tile_rows or not rows * space_count == size_y == size_z or steps * rows % 256:
         return False
     states = (time_count + 1) * band * rows * space_count * size_z
     return 4 * (3 * field.size + states) < 60 * 2**20

time: 734 us -> 732 us (level)
  no operation moved by 1% of the time
where the time goes in v4:
time: 732 us; the launch traced here: 731 us
  Pallas kernels  731 us (100%)
    pallas_call x1, Pallas kernels, fused_solve(): pl.pallas_call(functools.partial(fused_kernel, space_count, time_count, c...  725 us

profile of v4, /device:TPU:9, one launch (start us, length us, event | category | flops | bytes accessed | tf_op | source)
XLA Modules:
  0.0 731.4 jit_solution(5316841787653966411)
XLA Ops:
  0.0 0.0 copy-start
  0.0 0.0 copy-start.1
  0.0 725.5 %shard_map.73.in_ref = f32[256,128,128]{2,1,0:T(8,128)S(1)} custom-call(f32[256,128,128]{2,1,0:T(8,128)} %bitcast.5, f32[128,128]{1,0:T(8,128)} %vx_ref.1, f32[128,128]{1,0:T(8,128)} %left_ref.1, f32[128,128]{1,0:T(8,128)} %right_ref.1, f32[1,128]{1,0:T(1,128)} %bitcast.6, f32[1,128]{1,0:T(1,128)} %bitcast.7, f32[1,128]{1,0:T(1,128)} %bitcast.8), custom_call_target="tpu_custom_call" | custom-call | tf_op jit(solution)/shard_map/pallas_call | solution.py:373
  725.5 0.0 copy-done
  725.5 0.0 copy-done.1
  725.5 5.9 shard_map.74
Async XLA Ops:
  0.0 725.5 %copy-start = (f32[128,128]{1,0:T(8,128)S(1)}, f32[128,128]{1,0:T(8,128)}, u32[]{:S(2)}) copy-start(f32[128,128]{1,0:T(8,128)} %left_ref.1) | copy-start | bytes 196612
  0.0 725.5 %copy-start.1 = (f32[128,128]{1,0:T(8,128)S(1)}, f32[128,128]{1,0:T(8,128)}, u32[]{:S(2)}) copy-start(f32[128,128]{1,0:T(8,128)} %right_ref.1) | copy-start | bytes 196612

commit v5 on v4

--- a/solution.py
+++ b/solution.py
@@ -85,7 +85,7 @@
 def shrinking(total):
     if total % 256:
         return [total]
-    return [total // 256 * share for share in (160, 64, 16, 16)]
+    return [total // 256 * share for share in (160, 64, 32)]
 
 
 def transform_planes(source, target, start, count, left, right, shift=0):
@@ -342,7 +342,7 @@
     vmem = pl.BlockSpec(memory_space=pltpu.VMEM)
     held = shrinking(planes.shape[0])[-1]
     done = planes.shape[0] - held
-    pieces = 6 if done % 6 == 0 else 1
+    pieces = 7 if done % 7 == 0 else 1
     return pl.pallas_call(
         closing_kernel,
         in_specs=[vmem] * 3,

time: 732 us -> 731 us (level)
  no operation moved by 1% of the time
where the time goes in v5:
time: 731 us
  Pallas kernels  731 us (100%)
    pallas_call x1, Pallas kernels, fused_solve(): pl.pallas_call(functools.partial(fused_kernel, space_count, time_count, c...  725 us

profile of v5, /device:TPU:9, one launch (start us, length us, event | category | flops | bytes accessed | tf_op | source)
XLA Modules:
  0.0 731.3 jit_solution(16407218809375332326)
XLA Ops:
  0.0 0.0 copy-start
  0.0 0.0 copy-start.1
  0.0 725.3 %shard_map.73.in_ref = f32[256,128,128]{2,1,0:T(8,128)S(1)} custom-call(f32[256,128,128]{2,1,0:T(8,128)} %bitcast.5, f32[128,128]{1,0:T(8,128)} %vx_ref.1, f32[128,128]{1,0:T(8,128)} %left_ref.1, f32[128,128]{1,0:T(8,128)} %right_ref.1, f32[1,128]{1,0:T(1,128)} %bitcast.6, f32[1,128]{1,0:T(1,128)} %bitcast.7, f32[1,128]{1,0:T(1,128)} %bitcast.8), custom_call_target="tpu_custom_call" | custom-call | tf_op jit(solution)/shard_map/pallas_call | solution.py:373
  725.3 0.0 copy-done
  725.3 0.0 copy-done.1
  725.3 5.9 shard_map.74
Async XLA Ops:
  0.0 725.3 %copy-start = (f32[128,128]{1,0:T(8,128)S(1)}, f32[128,128]{1,0:T(8,128)}, u32[]{:S(2)}) copy-start(f32[128,128]{1,0:T(8,128)} %left_ref.1) | copy-start | bytes 196612
  0.0 725.3 %copy-start.1 = (f32[128,128]{1,0:T(8,128)S(1)}, f32[128,128]{1,0:T(8,128)}, u32[]{:S(2)}) copy-start(f32[128,128]{1,0:T(8,128)} %right_ref.1) | copy-start | bytes 196612
